TPU v7x, 32 devices: a whole 2x2x4 slice. The times are simulated.
32 devices in a mesh: band: 8 (over y, x, core), grid: 4 (over z).
Axes of the slice: x: 2, y: 2, z: 4, core: 2. Of those that a mesh axis runs over, the one named last changes fastest.
Arguments:
- wave: bfloat16 [4096, 10240], P('band', 'grid'), may hold values from -6 to 6
- ritz: bfloat16 [4096, 4096], P('band', 'grid'), may hold values from -0.125 to 0.125
- occupation: float32 [4096], P('band'), may hold values from 0 to 2
Outputs:
- rotated: bfloat16 [4096, 10240], P('band', 'grid')
- density: float32 [10240], P('grid')
All inputs are finite; a program needn't handle non-finite values.
Results may differ from a plain program's by a relative error of at most 0.0017.
Values may be sent and summed in bfloat16 or wider, within the bound.
A program may use at most 128 MiB of HBM per device.

v0:
```python
import jax
import jax.numpy as jnp
from jax import lax
from jax.sharding import PartitionSpec as P

NB = 4096


def per_device(wave, ritz, occupation):
    ritz_rows = lax.all_gather(ritz, "grid", axis=1, tiled=True)
    ritz_cols = lax.all_to_all(ritz_rows, "band", split_axis=1, concat_axis=0, tiled=True)
    summed = lax.dot_general(
        ritz_cols,
        lax.all_gather(wave, "band", axis=0, tiled=True),
        (((0,), (0,)), ((), ())),
        preferred_element_type=jnp.float32,
    )
    rotated = summed.astype(jnp.bfloat16)
    values = rotated.astype(jnp.float32)
    partial_terms = jnp.sum(occupation[:, None] * values * values, axis=0)
    density = lax.psum(partial_terms, "band") / NB
    return (rotated, density)


def solution(mesh):
    return jax.shard_map(
        per_device,
        mesh=mesh,
        in_specs=(P("band", "grid"), P("band", "grid"), P("band")),
        out_specs=(P("band", "grid"), P("grid")),
        check_vma=False,
    )
```

profile of v0, /device:TPU:0, one launch (start us, length us, event | category | flops | bytes accessed | tf_op | source)
XLA Modules:
  0.0 287.0 jit_solution(8882897534836297578)
XLA Ops:
  7.2 0.0 all-gather.3.cloned.1.call-start
  7.2 2.3 copy.5
  9.5 0.0 all-gather.3.cloned.1.call-update
  9.5 0.0 all-gather.5.cloned.1.call-start
  9.6 0.7 all-gather.5.cloned.1.call-update
  10.3 83.3 %all-gather.3.cloned.1.call-done = bf16[512,4096]{0,1:T(8,128)(2,1)} async-done(((bf16[512,1024]{0,1:T(8,128)(2,1)}), bf16[512,4096]{0,1:T(8,128)(2,1)}) %all-gather.3.cloned.1.call-update) | async-done | bytes 4194320 | tf_op jit(solution)/shard_map/all_gather | solution.py:10
  93.6 81.7 %all_to_all.19 = bf16[512,8,512]{0,2,1:T(8,128)(2,1)} all-to-all(bf16[512,8,512]{0,2,1:T(8,128)(2,1)} %bitcast.6), channel_id=1, replica_groups=mesh['band'=8,'grid'=4] {'band'}, dimensions={1} | all-to-all | bytes 8388608 | tf_op jit(solution)/shard_map/all_to_all | solution.py:11
  175.3 0.0 copy-start
  175.3 6.8 %copy.6 = bf16[8,512,512]{2,1,0:T(8,128)(2,1)} copy(bf16[8,512,512]{1,2,0:T(8,128)(2,1)} %bitcast.5) | data formatting | bytes 8388608 | tf_op jit(solution)/shard_map/all_to_all | solution.py:11
  182.1 56.3 %all-gather.5.cloned.1.call-done = bf16[4096,2560]{1,0:T(8,128)(2,1)} async-done(((bf16[512,2560]{1,0:T(8,128)(2,1)}), bf16[4096,2560]{1,0:T(8,128)(2,1)}) %all-gather.5.cloned.1.call-update) | async-done | bytes 20971536 | tf_op jit(solution)/shard_map/all_gather | solution.py:14
  238.4 0.0 copy-done
  238.4 17.7 %fusion = (f32[2560]{0:T(1024)S(1)}, bf16[512,2560]{1,0:T(8,128)(2,1)}) fusion(f32[512]{0:T(512)S(1)} %copy-done, bf16[4096,512]{1,0:T(8,128)(2,1)} %bitcast.7, bf16[4096,2560]{1,0:T(8,128)(2,1)} %all-gather.5.cloned.1.call-done), kind=kOutput, calls=%fused_computation.1 | convolution fusion | flops 10743969792 | bytes 27799552 | tf_op jit(solution)/shard_map/dot_general | solution.py:12
  256.1 23.5 %psum.7 = f32[2560]{0:T(1024)S(1)} all-reduce(f32[2560]{0:T(1024)S(1)} %get-tuple-element.2), channel_id=1, replica_groups=mesh['band'=8,'grid'=4] {'band'}, use_global_device_ids=true, to_apply=%region_1.0 | all-reduce | flops 2560 | bytes 20480 | tf_op jit(solution)/shard_map/psum | solution.py:21
  279.5 0.6 broadcast_multiply_fusion
Async XLA Ops:
  7.2 86.4 %all-gather.3.cloned.1.call-start = ((), (), s32[]{:S(2)}) async-start(), calls=%async_computation.1 | async-start | bytes 5242880 | tf_op jit(solution)/shard_map/all_gather | solution.py:10
  9.5 228.9 %all-gather.5.cloned.1.call-start = ((), (), s32[]{:S(2)}) async-start(), calls=%async_computation.2 | async-start | bytes 23592960 | tf_op jit(solution)/shard_map/all_gather | solution.py:14
  175.3 63.1 %copy-start = (f32[512]{0:T(512)S(1)}, f32[512]{0:T(512)}, u32[]{:S(2)}) copy-start(f32[512]{0:T(512)} %param.5) | copy-start | bytes 6148
Sparse Core Ops, SparseCore 0:
  10.1 83.4 all-gather.2
  95.5 142.8 all-gather.4
where the time goes:
time: 287 us
  waiting for transfers between devices  140 us (49%)
  blocking collectives  105 us (37%)
  matrix products  17.7 us (6%)
  between operations  14 us (5%)
  local copies, waits for them, and re-layouts  9.09 us (3%)
    all_gather x1, waiting for transfers between devices, per_device(): ritz_rows = lax.all_gather(ritz, 'grid', axis=1, tiled=True)  83.3 us
    all_to_all x1, blocking collectives, per_device(): lax.all_to_all(ritz_rows, 'band', split_axis=1, concat_axis=0, tiled=True)  81.7 us
    all_gather x1, waiting for transfers between devices, per_device(): lax.all_gather(wave, 'band', axis=0, tiled=True)  56.3 us
    psum x1, blocking collectives, per_device(): density = lax.psum(partial_terms, 'band') / NB  23.5 us
    dot_general x1, matrix products, per_device(): lax.dot_general(ritz_cols, lax.all_gather(wave, 'band', axis=0, tiled=Tru...  17.7 us
    all_to_all x1, local copies, waits for them, and re-layouts, per_device(): lax.all_to_all(ritz_rows, 'band', split_axis=1, concat_axis=0, tiled=True)  6.81 us
  transfers between devices with their start and end apart: 2, of which 2 were waited for; matrix products, arithmetic and copies ran while one was open for 2% of the time, Pallas kernels for 0%

commit v1 on v0

v1 whole, which is shorter than its diff:
```python
import functools

import jax
import jax.numpy as jnp
from jax import lax
from jax.experimental import pallas as pl
from jax.experimental.pallas import tpu as pltpu
from jax.sharding import PartitionSpec as P

MESH = pl.DeviceIdType.MESH
CHUNKS = 4


def chip_at(p, chips):
    p = lax.rem(p + chips, chips)
    back = (2 * p) // chips
    return (1 - back) * (2 * p) + back * (2 * (chips - 1 - p) + 1)


def kernel(
    nb, ng, wave, ritz, occ, rotated, density,
    w_all, z_all, a_buf, z_t, total, out_buf, d_all,
    a_send, a_recv, b_send, b_recv, up_send, dn_send, z_recv,
    r_send, l_send, d_send, w_recv, q_send, q_recv, o_sem,
):
    chips = nb // 2
    half = chips // 2
    rows, cells = wave.shape
    cols = z_all.shape[1]
    quarter = rows // ng
    crows = rows // CHUNKS
    me = lax.axis_index("band")
    g = lax.axis_index("grid")
    core = lax.rem(me, 2)
    chip = me // 2
    odd = lax.rem(chip, 2)
    place = (1 - odd) * (chip // 2) + odd * (chips - 1 - chip // 2)
    partner = me + 1 - 2 * core

    barrier = pltpu.get_barrier_semaphore()
    for d in range(1, nb):
        pl.semaphore_signal(barrier, inc=1, device_id={"band": lax.rem(me + d, nb), "grid": g}, device_id_type=MESH)
    for d in range(1, ng):
        pl.semaphore_signal(barrier, inc=1, device_id={"band": me, "grid": lax.rem(g + d, ng)}, device_id_type=MESH)
    pl.semaphore_wait(barrier, nb - 1 + ng - 1)

    def remote(src, dst, send, recv, band, grid):
        return pltpu.make_async_remote_copy(
            src_ref=src, dst_ref=dst, send_sem=send, recv_sem=recv,
            device_id={"band": band, "grid": grid}, device_id_type=MESH,
        )

    def a_copy(to):
        return remote(
            ritz.at[pl.ds(pl.multiple_of(to * quarter, quarter), quarter), :],
            a_buf.at[g], a_send.at[to], a_recv.at[g], me, to,
        )

    for d in range(1, ng):
        a_copy(lax.rem(g + d, ng)).start()
    a_own = pltpu.make_async_copy(
        ritz.at[pl.ds(pl.multiple_of(g * quarter, quarter), quarter), :], a_buf.at[g], a_recv.at[g]
    )
    a_own.start()

    def slot(band, ch):
        return w_all.at[pl.ds(pl.multiple_of(band * rows + ch * crows, crows), crows), :]

    def own_chunk(ch):
        return wave.at[pl.ds(ch * crows, crows), :]

    def ring_copy(step, d, ch):
        band = chip_at(place - step * d, chips) * 2 + core
        to = chip_at(place + step, chips) * 2 + core
        sems = r_send if step > 0 else l_send
        src = own_chunk(ch) if d == 0 else slot(band, ch)
        return remote(src, slot(band, ch), sems.at[d, ch], w_recv.at[band, ch], to, g)

    def pair_copy(band, ch, first):
        src = own_chunk(ch) if first else slot(band, ch)
        return remote(src, slot(band, ch), d_send.at[band // 2, ch], w_recv.at[band, ch], partner, g)

    low = list(range(CHUNKS // 2))
    high = list(range(CHUNKS // 2, CHUNKS))
    for a, b in zip(low, high):
        ring_copy(1, 0, a).start()
        ring_copy(-1, 0, b).start()
    for ch in range(CHUNKS):
        pltpu.make_async_copy(own_chunk(ch), slot(me, ch), w_recv.at[me, ch]).start()
        pair_copy(me, ch, True).start()

    def piece(band, q):
        return z_all.at[pl.ds(pl.multiple_of(band * rows + q * quarter, quarter), quarter), :]

    def b_copy(c, k):
        return remote(
            a_buf.at[c, :, pl.ds(k * cols, cols)], piece(me, g),
            b_send.at[2 * c + k], b_recv.at[me], 2 * c + k, g,
        )

    def b_local(c, k):
        return pltpu.make_async_copy(a_buf.at[c, :, pl.ds(k * cols, cols)], piece(me, g), b_recv.at[me])

    for d in range(ng):
        c = lax.rem(g + d, ng)
        remote(a_buf.at[c], a_buf.at[c], a_send.at[c], a_recv.at[c], me, g).wait_recv()
        for k in range(2):
            @pl.when(2 * c + k == me)
            def _():
                b_local(c, k).start()

            @pl.when(2 * c + k != me)
            def _():
                b_copy(c, k).start()

    for a, b in zip(high, low):
        ring_copy(1, 0, a).start()
        ring_copy(-1, 0, b).start()

    def z_copy(step, q, j):
        sems = up_send if step > 0 else dn_send
        return remote(piece(j, q), piece(j, q), sems.at[q, j], z_recv.at[q, j], me, g + step)

    def z_own(t, carry):
        j = lax.rem(me + t, nb)
        remote(piece(j, g), piece(j, g), b_send.at[j], b_recv.at[j], me, g).wait_recv()

        @pl.when(g < ng - 1)
        def _():
            z_copy(1, g, j).start()

        @pl.when(g > 0)
        def _():
            z_copy(-1, g, j).start()

        return carry

    lax.fori_loop(0, nb, z_own, 0)

    def z_step(t, carry):
        d = t // nb + 1
        j = lax.rem(me + t, nb)

        @pl.when(g - d >= 0)
        def _():
            z_copy(1, g - d, j).wait_recv()

            @pl.when(g < ng - 1)
            def _():
                z_copy(1, g - d, j).start()

        @pl.when(g + d < ng)
        def _():
            z_copy(-1, g + d, j).wait_recv()

            @pl.when(g > 0)
            def _():
                z_copy(-1, g + d, j).start()

        return carry

    events = []
    for d in range(1, half):
        events += [(d, a, b) for a, b in zip(low + high, high + low)]
    events += [(half, a, b) for a, b in zip(low, high)]

    def arrive(step, d, ch):
        band = chip_at(place - step * d, chips) * 2 + core
        ring_copy(step, d, ch).wait_recv()
        pair_copy(band, ch, False).start()
        mine = low if step > 0 else high
        if d + 1 < half or (d + 1 == half and ch in mine):
            ring_copy(step, d, ch).start()

    def wait_pair(band, ch):
        pair_copy(band, ch, False).wait_recv()

    tile = max(t for t in range(128, 513, 128) if cells % t == 0)
    depth = 2 * rows

    def load_t(c):
        z_t[...] = z_all[pl.ds(pl.multiple_of(c * depth, depth), depth), :].T

    def product(c, at):
        return jnp.dot(
            z_t[...], w_all[pl.ds(pl.multiple_of(c * depth, depth), depth), at],
            preferred_element_type=jnp.float32,
        )

    def add_chip(c, first):
        load_t(c)

        @pl.loop(0, cells // tile)
        def _(i):
            at = pl.ds(pl.multiple_of(i * tile, tile), tile)
            if first:
                total[:, at] = product(c, at)
            else:
                total[:, at] += product(c, at)

    steps = (ng - 1) * nb
    spread = len(events) - 1
    for e, (d, a, b) in enumerate(events):
        if e == spread:
            for ch in range(CHUNKS):
                remote(slot(me, ch), slot(me, ch), d_send.at[chip, ch], w_recv.at[me, ch], me, g).wait_recv()
                wait_pair(partner, ch)
            add_chip(chip, True)
            for dd in range(1, half):
                for step in (1, -1):
                    c = chip_at(place - step * dd, chips)
                    for ch in range(CHUNKS):
                        wait_pair(2 * c + 1 - core, ch)
                    add_chip(c, False)
        else:
            lax.fori_loop(steps * e // spread, steps * (e + 1) // spread, z_step, 0)
        arrive(1, d, a)
        arrive(-1, d, b)

    last = chip_at(place + half, chips)
    load_t(last)
    for ch in range(CHUNKS):
        wait_pair(2 * last + 1 - core, ch)

    @pl.loop(0, cells // tile)
    def _(i):
        at = pl.ds(pl.multiple_of(i * tile, tile), tile)
        rounded = (total[:, at] + product(last, at)).astype(jnp.bfloat16)
        out_buf[:, at] = rounded
        values = rounded.astype(jnp.float32)
        d_all[me, :, at] = jnp.sum(occ[...] * values * values, axis=0, keepdims=True)
        pltpu.make_async_copy(out_buf.at[:, at], rotated.at[:, at], o_sem.at[i]).start()

    def q_copy(to):
        return remote(d_all.at[me], d_all.at[me], q_send.at[to], q_recv.at[me], to, g)

    for d in range(1, nb):
        q_copy(lax.rem(me + d, nb)).start()

    for d in range(1, ng):
        a_copy(lax.rem(g + d, ng)).wait_send()

    def b_sent(to, carry):
        @pl.when(to != me)
        def _():
            remote(
                a_buf.at[0, :, pl.ds(0, cols)], piece(me, g), b_send.at[to], b_recv.at[me], to, g
            ).wait_send()

        return carry

    lax.fori_loop(0, nb, b_sent, 0)

    def z_sent(t, carry):
        q, j = t // nb, lax.rem(t, nb)

        @pl.when((q <= g) & (g < ng - 1))
        def _():
            z_copy(1, q, j).wait_send()

        @pl.when((q >= g) & (g > 0))
        def _():
            z_copy(-1, q, j).wait_send()

        return carry

    lax.fori_loop(0, ng * nb, z_sent, 0)
    for step in (1, -1):
        mine = low if step > 0 else high
        for d in range(half):
            for ch in (range(CHUNKS) if d + 1 < half else mine):
                ring_copy(step, d, ch).wait_send()
    for c in range(chips):
        for ch in range(CHUNKS):
            remote(slot(2 * c + core, ch), slot(2 * c + core, ch), d_send.at[c, ch], w_recv.at[2 * c + core, ch], partner, g).wait_send()

    for d in range(1, nb):
        src = lax.rem(me + d, nb)
        remote(d_all.at[src], d_all.at[src], q_send.at[src], q_recv.at[src], me, g).wait_recv()
    density[...] = jnp.sum(d_all[...], axis=0) / (nb * rows)
    for d in range(1, nb):
        q_copy(lax.rem(me + d, nb)).wait_send()

    @pl.loop(0, cells // tile)
    def _(i):
        at = pl.ds(pl.multiple_of(i * tile, tile), tile)
        pltpu.make_async_copy(out_buf.at[:, at], rotated.at[:, at], o_sem.at[i]).wait()


def solution(mesh):
    nb, ng = mesh.shape["band"], mesh.shape["grid"]

    def per_device(wave, ritz, occupation):
        rows, cells = wave.shape
        bands = rows * nb
        wide = ritz.shape[1]
        cols = bands // nb
        chips = nb // 2
        half = chips // 2
        dma = pltpu.SemaphoreType.DMA
        rotated, density = pl.pallas_call(
            functools.partial(kernel, nb, ng),
            out_shape=(
                jax.ShapeDtypeStruct((cols, cells), jnp.bfloat16),
                jax.ShapeDtypeStruct((1, cells), jnp.float32),
            ),
            in_specs=[
                pl.BlockSpec(memory_space=pl.ANY),
                pl.BlockSpec(memory_space=pl.ANY),
                pl.BlockSpec(memory_space=pltpu.VMEM),
            ],
            out_specs=(pl.BlockSpec(memory_space=pl.ANY), pl.BlockSpec(memory_space=pltpu.VMEM)),
            scratch_shapes=[
                pltpu.VMEM((bands, cells), jnp.bfloat16),
                pltpu.VMEM((bands, cols), jnp.bfloat16),
                pltpu.VMEM((ng, rows // ng, wide), jnp.bfloat16),
                pltpu.VMEM((cols, 2 * rows), jnp.bfloat16),
                pltpu.VMEM((cols, cells), jnp.float32),
                pltpu.VMEM((cols, cells), jnp.bfloat16),
                pltpu.VMEM((nb, 1, cells), jnp.float32),
                dma((ng,)), dma((ng,)), dma((nb,)), dma((nb,)),
                dma((ng, nb)), dma((ng, nb)), dma((ng, nb)),
                dma((half, CHUNKS)), dma((half, CHUNKS)), dma((chips, CHUNKS)), dma((nb, CHUNKS)),
                dma((nb,)), dma((nb,)), dma((cells // 128,)),
            ],
            compiler_params=pltpu.CompilerParams(
                collective_id=0, has_side_effects=True, vmem_limit_bytes=60 * 1024 * 1024
            ),
        )(wave, ritz, occupation[:, None])
        return rotated, density.reshape(cells)

    return jax.shard_map(
        per_device,
        mesh=mesh,
        in_specs=(P("band", "grid"), P("band", "grid"), P("band")),
        out_specs=(P("band", "grid"), P("grid")),
        check_vma=False,
    )
```

time: 287 us -> 142 us (0.49)
  waiting for transfers between devices: 140 us -> 0 us
  Pallas kernels: 0 us -> 135 us
  blocking collectives: 105 us -> 0 us
  matrix products: 17.7 us -> 0 us
  between operations: 14 us -> 0.64 us
  local copies, waits for them, and re-layouts: 9.09 us -> 4.93 us
    all_gather x2 -> x0, waiting for transfers between devices: 140 us -> none  [the longest x1 83.3 us: per_device(): ritz_rows = lax.all_gather(ritz, 'grid', axis=1, tiled=True)]
    pallas_call x0 -> x1, Pallas kernels: none -> 135 us  [per_device(): pl.pallas_call(functools.partial(kernel, nb, ng), out_shape=(jax.ShapeDty...]
    all_to_all x1 -> x0, blocking collectives: 81.7 us -> none  [per_device(): lax.all_to_all(ritz_rows, 'band', split_axis=1, concat_axis=0, tiled=True)]
    psum x1 -> x0, blocking collectives: 23.5 us -> none  [per_device(): density = lax.psum(partial_terms, 'band') / NB]
    dot_general x1 -> x0, matrix products: 17.7 us -> none  [per_device(): lax.dot_general(ritz_cols, lax.all_gather(wave, 'band', axis=0, tiled=Tru...]
    all_to_all x1 -> x0, local copies, waits for them, and re-layouts: 6.81 us -> none  [per_device(): lax.all_to_all(ritz_rows, 'band', split_axis=1, concat_axis=0, tiled=True)]
  transfers between devices with their start and end apart: 2 -> 0, of which waited for: 2 -> 0; matrix products, arithmetic and copies ran while one was open for 2% -> 0% of each run, Pallas kernels for 0% -> 0%
where the time goes in v1:
time: 142 us
  Pallas kernels  135 us (95%)
  local copies, waits for them, and re-layouts  4.93 us (3%)
    pallas_call x1, Pallas kernels, per_device(): pl.pallas_call(functools.partial(kernel, nb, ng), out_shape=(jax.ShapeDty...  135 us
    unnamed x1, local copies, waits for them, and re-layouts  3.4 us

profile of v1, /device:TPU:0, one launch (start us, length us, event | category | flops | bytes accessed | tf_op | source)
XLA Modules:
  0.0 141.9 jit_solution(11819358799421176340)
XLA Ops:
  0.6 1.5 %copy.5.occ = f32[512,1]{1,0:T(8,128)} copy(f32[512,1]{0,1:T(1,128)} %bitcast.1) | data formatting | bytes 4096 | tf_op jit(solution)/shard_map/broadcast_in_dim | solution.py:329
  2.2 135.0 %shard_map.50 = (bf16[512,2560]{1,0:T(8,128)(2,1)}, f32[1,2560]{1,0:T(1,128)}) custom-call(bf16[512,2560]{1,0:T(8,128)(2,1)} %wave.1, bf16[512,1024]{1,0:T(8,128)(2,1)} %ritz.1, f32[512,1]{1,0:T(8,128)} %copy.5.occ), custom_call_target="tpu_custom_call" | custom-call | tf_op jit(solution)/shard_map/pallas_call | solution.py:301
  137.2 1.3 reduce
  138.5 3.4 %copy.7 = bf16[512,2560]{1,0:T(8,128)(2,1)} copy(bf16[512,2560]{1,0:T(8,128)(2,1)} %get-tuple-element.8) | data formatting | bytes 5242880

commit v2 on v1

--- a/solution.py
+++ b/solution.py
@@ -8,7 +8,7 @@
 from jax.sharding import PartitionSpec as P
 
 MESH = pl.DeviceIdType.MESH
-CHUNKS = 4
+CHUNKS = 8
 
 
 def chip_at(p, chips):
@@ -19,7 +19,7 @@
 
 def kernel(
     nb, ng, wave, ritz, occ, rotated, density,
-    w_all, z_all, a_buf, z_t, total, out_buf, d_all,
+    w_all, z_all, a_buf, z_t, total, out_buf, d_all, o_col,
     a_send, a_recv, b_send, b_recv, up_send, dn_send, z_recv,
     r_send, l_send, d_send, w_recv, q_send, q_recv, o_sem,
 ):
@@ -82,9 +82,15 @@
 
     low = list(range(CHUNKS // 2))
     high = list(range(CHUNKS // 2, CHUNKS))
-    for a, b in zip(low, high):
-        ring_copy(1, 0, a).start()
-        ring_copy(-1, 0, b).start()
+    waiting = list(zip(low + high, high + low))
+
+    def send_own(count):
+        for _ in range(min(count, len(waiting))):
+            a, b = waiting.pop(0)
+            ring_copy(1, 0, a).start()
+            ring_copy(-1, 0, b).start()
+
+    send_own(1)
     for ch in range(CHUNKS):
         pltpu.make_async_copy(own_chunk(ch), slot(me, ch), w_recv.at[me, ch]).start()
         pair_copy(me, ch, True).start()
@@ -113,9 +119,9 @@
             def _():
                 b_copy(c, k).start()
 
-    for a, b in zip(high, low):
-        ring_copy(1, 0, a).start()
-        ring_copy(-1, 0, b).start()
+        send_own(1)
+    send_own(CHUNKS)
+    o_col[...] = jnp.broadcast_to(occ[...], (128, cols)).T
 
     def z_copy(step, q, j):
         sems = up_send if step > 0 else dn_send
@@ -178,57 +184,82 @@
     tile = max(t for t in range(128, 513, 128) if cells % t == 0)
     depth = 2 * rows
 
-    def load_t(c):
-        z_t[...] = z_all[pl.ds(pl.multiple_of(c * depth, depth), depth), :].T
-
-    def product(c, at):
-        return jnp.dot(
-            z_t[...], w_all[pl.ds(pl.multiple_of(c * depth, depth), depth), at],
-            preferred_element_type=jnp.float32,
+    depth2 = 2 * quarter
+
+    def wait_chip(c):
+        for ch in range(CHUNKS):
+            wait_pair(2 * c + 1 - core, ch)
+
+    def both(ref, c, q, at):
+        return jnp.concatenate(
+            [ref[pl.ds(pl.multiple_of((2 * c + k) * rows + q * quarter, quarter), quarter), at] for k in range(2)]
         )
 
-    def add_chip(c, first):
-        load_t(c)
+    def add_quarter(c, q, first=False):
+        z_t[:, :depth2] = both(z_all, c, q, slice(None)).T
 
         @pl.loop(0, cells // tile)
         def _(i):
             at = pl.ds(pl.multiple_of(i * tile, tile), tile)
+            term = jnp.dot(z_t[:, :depth2], both(w_all, c, q, at), preferred_element_type=jnp.float32)
             if first:
-                total[:, at] = product(c, at)
+                total[:, at] = term
             else:
-                total[:, at] += product(c, at)
+                total[:, at] += term
+
+    def add_unit(c, dz):
+        if dz == 0:
+            add_quarter(c, g)
+            return
+
+        @pl.when(g - dz >= 0)
+        def _():
+            add_quarter(c, g - dz)
+
+        @pl.when(g + dz < ng)
+        def _():
+            add_quarter(c, g + dz)
+
+    for ch in range(CHUNKS):
+        remote(slot(me, ch), slot(me, ch), d_send.at[chip, ch], w_recv.at[me, ch], me, g).wait_recv()
+        wait_pair(partner, ch)
+    add_quarter(chip, g, True)
 
     steps = (ng - 1) * nb
-    spread = len(events) - 1
+    spread = len(events)
+    done = {(0, 0)}
     for e, (d, a, b) in enumerate(events):
-        if e == spread:
-            for ch in range(CHUNKS):
-                remote(slot(me, ch), slot(me, ch), d_send.at[chip, ch], w_recv.at[me, ch], me, g).wait_recv()
-                wait_pair(partner, ch)
-            add_chip(chip, True)
-            for dd in range(1, half):
-                for step in (1, -1):
-                    c = chip_at(place - step * dd, chips)
-                    for ch in range(CHUNKS):
-                        wait_pair(2 * c + 1 - core, ch)
-                    add_chip(c, False)
-        else:
-            lax.fori_loop(steps * e // spread, steps * (e + 1) // spread, z_step, 0)
+        lax.fori_loop(steps * e // spread, steps * (e + 1) // spread, z_step, 0)
         arrive(1, d, a)
         arrive(-1, d, b)
+        for dd in range(half):
+            if dd > (e + 1) // CHUNKS:
+                continue
+            for dz in range(ng):
+                if (dd, dz) in done or nb * dz > steps * (e + 1) // spread:
+                    continue
+                done.add((dd, dz))
+                for step in (1, -1) if dd else (1,):
+                    c = chip_at(place - step * dd, chips)
+                    if dd and not any((dd, x) in done for x in range(dz)):
+                        wait_chip(c)
+                    add_unit(c, dz)
 
     last = chip_at(place + half, chips)
-    load_t(last)
-    for ch in range(CHUNKS):
-        wait_pair(2 * last + 1 - core, ch)
+    depth = 2 * rows
+    last_rows = pl.ds(pl.multiple_of(last * depth, depth), depth)
+    z_t[...] = z_all[last_rows, :].T
+    occ_tile = jnp.concatenate([o_col[...]] * (tile // 128), axis=1)
+    wait_chip(last)
 
     @pl.loop(0, cells // tile)
     def _(i):
         at = pl.ds(pl.multiple_of(i * tile, tile), tile)
-        rounded = (total[:, at] + product(last, at)).astype(jnp.bfloat16)
+        term = jnp.dot(z_t[...], w_all[last_rows, at], preferred_element_type=jnp.float32)
+        rounded = (total[:, at] + term).astype(jnp.bfloat16)
         out_buf[:, at] = rounded
         values = rounded.astype(jnp.float32)
-        d_all[me, :, at] = jnp.sum(occ[...] * values * values, axis=0, keepdims=True)
+        d_all[me, :, at] = jnp.sum(occ_tile * values * values, axis=0, keepdims=True)
         pltpu.make_async_copy(out_buf.at[:, at], rotated.at[:, at], o_sem.at[i]).start()
 
     def q_copy(to):
@@ -277,7 +308,7 @@
     for d in range(1, nb):
         src = lax.rem(me + d, nb)
         remote(d_all.at[src], d_all.at[src], q_send.at[src], q_recv.at[src], me, g).wait_recv()
-    density[...] = jnp.sum(d_all[...], axis=0) / (nb * rows)
+    density[...] = jnp.sum(d_all[...], axis=(0, 1)) / (nb * rows)
     for d in range(1, nb):
         q_copy(lax.rem(me + d, nb)).wait_send()
 
@@ -302,7 +333,7 @@
             functools.partial(kernel, nb, ng),
             out_shape=(
                 jax.ShapeDtypeStruct((cols, cells), jnp.bfloat16),
-                jax.ShapeDtypeStruct((1, cells), jnp.float32),
+                jax.ShapeDtypeStruct((cells,), jnp.float32),
             ),
             in_specs=[
                 pl.BlockSpec(memory_space=pl.ANY),
@@ -318,6 +349,7 @@
                 pltpu.VMEM((cols, cells), jnp.float32),
                 pltpu.VMEM((cols, cells), jnp.bfloat16),
                 pltpu.VMEM((nb, 1, cells), jnp.float32),
+                pltpu.VMEM((cols, 128), jnp.float32),
                 dma((ng,)), dma((ng,)), dma((nb,)), dma((nb,)),
                 dma((ng, nb)), dma((ng, nb)), dma((ng, nb)),
                 dma((half, CHUNKS)), dma((half, CHUNKS)), dma((chips, CHUNKS)), dma((nb, CHUNKS)),
@@ -326,8 +358,8 @@
             compiler_params=pltpu.CompilerParams(
                 collective_id=0, has_side_effects=True, vmem_limit_bytes=60 * 1024 * 1024
             ),
-        )(wave, ritz, occupation[:, None])
-        return rotated, density.reshape(cells)
+        )(wave, ritz, occupation[None, :])
+        return rotated, density
 
     return jax.shard_map(
         per_device,

time: 142 us -> 140 us (0.986)
    broadcast_in_dim x1 -> x0, local copies, waits for them, and re-layouts: 1.53 us -> none  [per_device(): occupation[:, None]]
    unnamed x1 -> x4, local copies, waits for them, and re-layouts: 3.4 us -> 4.01 us
where the time goes in v2:
time: 140 us; the launch traced here: 139 us
  Pallas kernels  135 us (96%)
  local copies, waits for them, and re-layouts  4.01 us (3%)
    pallas_call x1, Pallas kernels, per_device(): pl.pallas_call(functools.partial(kernel, nb, ng), out_shape=(jax.ShapeDty...  135 us
    unnamed x4, local copies, waits for them, and re-layouts  4.01 us

profile of v2, /device:TPU:0, one launch (start us, length us, event | category | flops | bytes accessed | tf_op | source)
XLA Modules:
  0.0 139.3 jit_solution(12312863460734761965)
XLA Ops:
  0.6 134.7 %shard_map.50 = (bf16[512,2560]{1,0:T(8,128)(2,1)}, f32[2560]{0:T(1024)}) custom-call(bf16[512,2560]{1,0:T(8,128)(2,1)} %wave.1, bf16[512,1024]{1,0:T(8,128)(2,1)} %ritz.1, f32[1,512]{1,0:T(1,128)} %bitcast.1), custom_call_target="tpu_custom_call" | custom-call | tf_op jit(solution)/shard_map/pallas_call | solution.py:332
  135.3 0.0 copy-start
  135.3 3.4 %copy.7 = bf16[512,2560]{1,0:T(8,128)(2,1)} copy(bf16[512,2560]{1,0:T(8,128)(2,1)} %get-tuple-element.4) | data formatting | bytes 5242880
  138.7 0.0 copy-done
  138.7 0.6 copy.8
Async XLA Ops:
  135.3 3.4 %copy-start = (f32[2560]{0:T(1024)S(1)}, f32[2560]{0:T(1024)}, u32[]{:S(2)}) copy-start(f32[2560]{0:T(1024)} %get-tuple-element.5) | copy-start | bytes 30724

commit v3 on v2

--- a/solution.py
+++ b/solution.py
@@ -9,6 +9,8 @@
 
 MESH = pl.DeviceIdType.MESH
 CHUNKS = 8
+AHEAD = 3
+Z_AHEAD = 5
 
 
 def chip_at(p, chips):
@@ -82,15 +84,21 @@
 
     low = list(range(CHUNKS // 2))
     high = list(range(CHUNKS // 2, CHUNKS))
-    waiting = list(zip(low + high, high + low))
-
-    def send_own(count):
-        for _ in range(min(count, len(waiting))):
-            a, b = waiting.pop(0)
-            ring_copy(1, 0, a).start()
-            ring_copy(-1, 0, b).start()
-
-    send_own(1)
+    waiting = []
+    for d in range(half):
+        waiting += [(d, a, b) for a, b in zip(low + high, high + low)]
+    waiting = waiting[: (half - 1) * CHUNKS + CHUNKS // 2]
+    events = [(d + 1, a, b) for d, a, b in waiting]
+    sent = [0]
+
+    def send_until(count):
+        while sent[0] < min(count, len(waiting)):
+            d, a, b = waiting[sent[0]]
+            ring_copy(1, d, a).start()
+            ring_copy(-1, d, b).start()
+            sent[0] += 1
+
+    send_until(1)
     for ch in range(CHUNKS):
         pltpu.make_async_copy(own_chunk(ch), slot(me, ch), w_recv.at[me, ch]).start()
         pair_copy(me, ch, True).start()
@@ -119,29 +127,37 @@
             def _():
                 b_copy(c, k).start()
 
-        send_own(1)
-    send_own(CHUNKS)
+        if d == 0:
+            send_until(AHEAD)
     o_col[...] = jnp.broadcast_to(occ[...], (128, cols)).T
 
     def z_copy(step, q, j):
         sems = up_send if step > 0 else dn_send
         return remote(piece(j, q), piece(j, q), sems.at[q, j], z_recv.at[q, j], me, g + step)
 
-    def z_own(t, carry):
-        j = lax.rem(me + t, nb)
-        remote(piece(j, g), piece(j, g), b_send.at[j], b_recv.at[j], me, g).wait_recv()
-
-        @pl.when(g < ng - 1)
-        def _():
-            z_copy(1, g, j).start()
-
-        @pl.when(g > 0)
-        def _():
-            z_copy(-1, g, j).start()
-
+    steps = (ng - 1) * nb
+
+    def z_send(n):
+        d = n // nb
+        j = lax.rem(me + n, nb)
+
+        @pl.when(d == 0)
+        def _():
+            remote(piece(j, g), piece(j, g), b_send.at[j], b_recv.at[j], me, g).wait_recv()
+
+        @pl.when((g - d >= 0) & (g < ng - 1))
+        def _():
+            z_copy(1, g - d, j).start()
+
+        @pl.when((g + d < ng) & (g > 0))
+        def _():
+            z_copy(-1, g + d, j).start()
+
+    def z_first(n, carry):
+        z_send(n)
         return carry
 
-    lax.fori_loop(0, nb, z_own, 0)
+    lax.fori_loop(0, Z_AHEAD, z_first, 0)
 
     def z_step(t, carry):
         d = t // nb + 1
@@ -151,32 +167,20 @@
         def _():
             z_copy(1, g - d, j).wait_recv()
 
-            @pl.when(g < ng - 1)
-            def _():
-                z_copy(1, g - d, j).start()
-
         @pl.when(g + d < ng)
         def _():
             z_copy(-1, g + d, j).wait_recv()
 
-            @pl.when(g > 0)
-            def _():
-                z_copy(-1, g + d, j).start()
+        @pl.when(t + Z_AHEAD < steps)
+        def _():
+            z_send(t + Z_AHEAD)
 
         return carry
-
-    events = []
-    for d in range(1, half):
-        events += [(d, a, b) for a, b in zip(low + high, high + low)]
-    events += [(half, a, b) for a, b in zip(low, high)]
 
     def arrive(step, d, ch):
         band = chip_at(place - step * d, chips) * 2 + core
         ring_copy(step, d, ch).wait_recv()
         pair_copy(band, ch, False).start()
-        mine = low if step > 0 else high
-        if d + 1 < half or (d + 1 == half and ch in mine):
-            ring_copy(step, d, ch).start()
 
     def wait_pair(band, ch):
         pair_copy(band, ch, False).wait_recv()
@@ -207,9 +211,9 @@
             else:
                 total[:, at] += term
 
-    def add_unit(c, dz):
+    def add_unit(c, dz, first):
         if dz == 0:
-            add_quarter(c, g)
+            add_quarter(c, g, first)
             return
 
         @pl.when(g - dz >= 0)
@@ -223,27 +227,26 @@
     for ch in range(CHUNKS):
         remote(slot(me, ch), slot(me, ch), d_send.at[chip, ch], w_recv.at[me, ch], me, g).wait_recv()
         wait_pair(partner, ch)
-    add_quarter(chip, g, True)
-
-    steps = (ng - 1) * nb
+
     spread = len(events)
-    done = {(0, 0)}
+    done = set()
     for e, (d, a, b) in enumerate(events):
         lax.fori_loop(steps * e // spread, steps * (e + 1) // spread, z_step, 0)
         arrive(1, d, a)
         arrive(-1, d, b)
+        send_until(e + 1 + AHEAD)
         for dd in range(half):
             if dd > (e + 1) // CHUNKS:
                 continue
             for dz in range(ng):
-                if (dd, dz) in done or nb * dz > steps * (e + 1) // spread:
+                if (dd, dz) in done or max(nb * dz, nb - Z_AHEAD) > steps * (e + 1) // spread:
                     continue
                 done.add((dd, dz))
                 for step in (1, -1) if dd else (1,):
                     c = chip_at(place - step * dd, chips)
                     if dd and not any((dd, x) in done for x in range(dz)):
                         wait_chip(c)
-                    add_unit(c, dz)
+                    add_unit(c, dz, dd == 0)
 
     last = chip_at(place + half, chips)
     depth = 2 * rows

time: 140 us -> 129 us (0.921)
  Pallas kernels: 135 us -> 124 us
    pallas_call x1, Pallas kernels: 135 us -> 124 us  [per_device(): pl.pallas_call(functools.partial(kernel, nb, ng), out_shape=(jax.ShapeDty...]
where the time goes in v3:
time: 129 us; the launch traced here: 128 us
  Pallas kernels  124 us (96%)
  local copies, waits for them, and re-layouts  4.01 us (3%)
    pallas_call x1, Pallas kernels, per_device(): pl.pallas_call(functools.partial(kernel, nb, ng), out_shape=(jax.ShapeDty...  124 us
    unnamed x4, local copies, waits for them, and re-layouts  4.01 us

profile of v3, /device:TPU:0, one launch (start us, length us, event | category | flops | bytes accessed | tf_op | source)
XLA Modules:
  0.0 128.4 jit_solution(11166673483653433535)
XLA Ops:
  0.6 123.8 %shard_map.50 = (bf16[512,2560]{1,0:T(8,128)(2,1)}, f32[2560]{0:T(1024)}) custom-call(bf16[512,2560]{1,0:T(8,128)(2,1)} %wave.1, bf16[512,1024]{1,0:T(8,128)(2,1)} %ritz.1, f32[1,512]{1,0:T(1,128)} %bitcast.1), custom_call_target="tpu_custom_call" | custom-call | tf_op jit(solution)/shard_map/pallas_call | solution.py:335
  124.4 0.0 copy-start
  124.4 3.4 %copy.7 = bf16[512,2560]{1,0:T(8,128)(2,1)} copy(bf16[512,2560]{1,0:T(8,128)(2,1)} %get-tuple-element.4) | data formatting | bytes 5242880
  127.8 0.0 copy-done
  127.8 0.6 copy.8
Async XLA Ops:
  124.4 3.4 %copy-start = (f32[2560]{0:T(1024)S(1)}, f32[2560]{0:T(1024)}, u32[]{:S(2)}) copy-start(f32[2560]{0:T(1024)} %get-tuple-element.5) | copy-start | bytes 30724
